TPU v7x, 32 devices: a whole 2x2x4 slice. The times are simulated.
32 devices in a mesh: tp: 4 (over z), pp: 8 (over y, x, core).
Axes of the slice: x: 2, y: 2, z: 4, core: 2. Of those that a mesh axis runs over, the one named last changes fastest.
Arguments:
- tokens: bfloat16 [8192, 8192], P('pp', 'tp'), may hold values from -60 to 60
- norm_gain: bfloat16 [8192], P('tp'), may hold values from 0.099609375 to 1.8984375
- weights_gen: bfloat16 [8, 1280, 8192], P('tp', None, 'pp'), may hold values from -2 to 2
- segment_ids: int32 [8, 1024], P('pp'), may hold values from 0 to 15, never falling along the last dimension, each value on 1 to 512 neighbouring positions
Outputs:
- weights_rows: bfloat16 [8, 1280, 8192], P('tp', 'pp')
- attended: bfloat16 [8192, 8192], P('pp', 'tp')
Inputs may be any that keep to these rules, and one draw needn't show every extreme that they name: `segment_ids`: ids never fall along a block; every sequence has 1 to 512 tokens and lies in one block.
All inputs are finite; a program needn't handle non-finite values.
Results may differ from a plain program's by a relative error of at most 0.0075.
Values may be sent and summed in bfloat16 or wider, within the bound.
No kernel may reach another device: no remote copies, remote signals or barrier semaphores. Data moves between devices by JAX's collectives and lax.ppermute only.
A program may use at most 192 MiB of HBM per device.

v0:
```python
import math
import jax
import jax.numpy as jnp
from jax import lax
from jax.sharding import PartitionSpec as P

DH = 128
GROUP = 8
rope_base = 500000.0


def rotary(values, positions):
    half = values.shape[-1] // 2
    freq = jnp.exp(
        jnp.arange(half, dtype=jnp.float32) * (-2.0 * math.log(rope_base) / values.shape[-1])
    )
    angle = positions.astype(jnp.float32)[:, None] * freq[None, :]
    cosine = jnp.cos(angle)
    sine = jnp.sin(angle)
    extra = values.ndim - 2
    cosine = cosine.reshape(cosine.shape[:1] + (1,) * extra + cosine.shape[1:])
    sine = sine.reshape(sine.shape[:1] + (1,) * extra + sine.shape[1:])
    first = values[..., :half]
    second = values[..., half:]
    return jnp.concatenate(
        [first * cosine - second * sine, second * cosine + first * sine], axis=-1
    )


def shards(tokens, norm_gain, weights_gen, segment_ids):
    weights_rows = lax.all_to_all(weights_gen, "pp", split_axis=1, concat_axis=2, tiled=True)
    gathered, gain = (
        lax.all_gather(tokens, "tp", axis=1, tiled=True),
        lax.all_gather(norm_gain, "tp", axis=0, tiled=True),
    )
    floats = gathered.astype(jnp.float32)
    square = jnp.mean(floats * floats, axis=-1, keepdims=True)
    normed = (floats * lax.rsqrt(square + 1e-05) * gain.astype(jnp.float32)).astype(jnp.bfloat16)
    count = normed.shape[0]
    groups = weights_gen.shape[0]
    mixed = jnp.einsum(
        "td,grd->tgr",
        normed,
        lax.all_gather(weights_rows, "pp", axis=1, tiled=True),
        preferred_element_type=jnp.float32,
    )
    mixed = mixed.reshape(count, groups, GROUP + 2, DH)
    seg = segment_ids[0]
    order = jnp.arange(count, dtype=jnp.int32)
    start_index = jnp.sum((seg[None, :] < seg[:, None]).astype(jnp.int32), axis=1)
    positions = order - start_index
    query = rotary(mixed[:, :, :GROUP, :], positions).astype(jnp.bfloat16)
    key_heads = rotary(mixed[:, :, GROUP, :], positions).astype(jnp.bfloat16)
    value_heads = mixed[:, :, GROUP + 1, :].astype(jnp.bfloat16)
    score = jnp.einsum("tgjd,sgd->gjts", query, key_heads, preferred_element_type=jnp.float32) * (
        1.0 / math.sqrt(DH)
    )
    allowed = (seg[:, None] == seg[None, :]) & (order[:, None] >= order[None, :])
    score = jnp.where(allowed[None, None], score, -1e30)
    top = jnp.max(score, axis=-1, keepdims=True)
    expo = jnp.where(allowed[None, None], jnp.exp(score - top), 0.0)
    prob = (expo / jnp.sum(expo, axis=-1, keepdims=True)).astype(jnp.bfloat16)
    output = jnp.einsum("gjts,sgd->tgjd", prob, value_heads, preferred_element_type=jnp.float32)
    attended = output.astype(jnp.bfloat16).reshape(count, groups * GROUP * DH)
    return (weights_rows, attended)


def solution(mesh):
    in_specs = (P("pp", "tp"), P("tp"), P("tp", None, "pp"), P("pp", None))
    out_specs = (P("tp", "pp", None), P("pp", "tp"))
    return jax.shard_map(shards, mesh=mesh, in_specs=in_specs, out_specs=out_specs, check_vma=False)
```

profile of v0, /device:TPU:0, one launch (start us, length us, event | category | flops | bytes accessed | tf_op | source)
XLA Modules:
  0.0 658.1 jit_solution(8889944450149644430)
XLA Ops:
  7.2 0.7 all-gather.3.cloned.1.call-update
  7.9 0.0 all-gather.5.cloned.1.call-start
  7.9 9.4 %copy.21 = bf16[2,1280,1024]{2,0,1:T(2,128)(2,1)S(1)} copy(bf16[2,1280,1024]{2,1,0:T(8,128)(2,1)} %param.6) | data formatting | bytes 10485760 | tf_op args[2]
  17.4 65.3 %all_to_all.18 = bf16[2,1280,1024]{2,0,1:T(2,128)(2,1)S(1)} all-to-all(bf16[2,1280,1024]{2,0,1:T(2,128)(2,1)S(1)} %copy.21), channel_id=1, replica_groups=mesh['tp'=4,'pp'=8] {'pp'}, dimensions={1} | all-to-all | bytes 10485760 | tf_op jit(solution)/shard_map/all_to_all | solution.py:31
  82.6 5.2 copy.43
  87.8 8.9 %all_to_all.16 = bf16[2,160,8192]{2,1,0:T(8,128)(2,1)} reshape(bf16[2,160,8,1024]{3,2,1,0:T(8,128)(2,1)} %bitcast.49) | data formatting | bytes 10485760 | tf_op jit(solution)/shard_map/all_to_all | solution.py:31
  96.8 24.4 %all_gather.10 = bf16[8192]{0:T(1024)(128)(2,1)S(1)} all-gather(bf16[2048]{0:T(1024)(128)(2,1)S(1)} %copy-done.2), channel_id=1, replica_groups=mesh['tp'=4,'pp'=8] {'tp'}, dimensions={0}, use_global_device_ids=true | all-gather | bytes 20480 | tf_op jit(solution)/shard_map/all_gather | solution.py:34
  121.2 0.5 convert_reduce_fusion
  121.7 1.9 multiply_cosine_fusion
  123.6 1.6 fusion.16
  125.1 174.1 %all-gather.3.cloned.1.call-done = bf16[1024,8192]{1,0:T(8,128)(2,1)} async-done(((bf16[1024,2048]{1,0:T(8,128)(2,1)}), bf16[1024,8192]{1,0:T(8,128)(2,1)}) %all-gather.3.cloned.1.call-update) | async-done | bytes 16777232 | tf_op jit(solution)/shard_map/all_gather | solution.py:33
  299.3 7.2 %fusion.2 = f32[1024]{0:T(1024)S(1)} fusion(bf16[1024,8192]{1,0:T(8,128)(2,1)} %all-gather.3.cloned.1.call-done), kind=kLoop, calls=%fused_computation.7 | loop fusion | flops 25164800 | bytes 16781312 | tf_op jit(solution)/shard_map/reduce_sum | solution.py:37
  306.5 189.8 %all-gather.5.cloned.1.call-done = bf16[2,1280,8192]{2,1,0:T(8,128)(2,1)} async-done(((bf16[2,160,8192]{2,1,0:T(8,128)(2,1)}), bf16[2,1280,8192]{2,1,0:T(8,128)(2,1)}) %all-gather.5.cloned.1.call-update) | async-done | bytes 41943056 | tf_op jit(solution)/shard_map/all_gather | solution.py:44
  496.3 54.2 %fusion.10 = f32[1024,2,1280]{0,2,1:T(8,128)} fusion(bf16[2,1280,8192]{2,1,0:T(8,128)(2,1)} %all-gather.5.cloned.1.call-done, bf16[1024,8192]{1,0:T(8,128)(2,1)} %all-gather.3.cloned.1.call-done, f32[8192]{0:T(1024)S(1)} %convert_element_type.36, f32[1024]{0:T(1024)S(1)} %add_rsqrt_fusion), kind=kOutput, calls=%fused_computation.15 | convolution fusion | flops 42983227392 | bytes 69242880 | tf_op jit(solution)/shard_map/td,grd->tgr/dot_general | solution.py:41
  550.5 1.3 slice.29
  551.8 8.5 %fusion.27 = (f32[1024,2,8,64]{0,3,2,1:T(8,128)}, f32[1024,2,8,64]{0,3,2,1:T(8,128)}) fusion(f32[1024,2,10,128]{0,3,2,1:T(8,128)} %bitcast.52), kind=kLoop, calls=%fused_computation.42 | loop fusion | bytes 16777216 | tf_op jit(solution)/shard_map/slice | solution.py:24
  560.2 0.3 copy.34
  560.5 6.9 %copy.36 = f32[1024,2,8,64]{3,0,2,1:T(8,128)} copy(f32[1024,2,8,64]{0,3,2,1:T(8,128)} %get-tuple-element.10) | data formatting | bytes 8388608
  567.5 6.9 %copy.35 = f32[1024,2,8,64]{3,0,2,1:T(8,128)} copy(f32[1024,2,8,64]{0,3,2,1:T(8,128)} %get-tuple-element.11) | data formatting | bytes 8388608
  574.3 0.4 subtract_convert_fusion.1
  574.8 9.6 %subtract_convert_fusion = (bf16[1024,2,8,64]{3,0,2,1:T(8,128)(2,1)}, bf16[1024,2,8,64]{3,0,2,1:T(8,128)(2,1)}) fusion(f32[1024,2,8,64]{3,0,2,1:T(8,128)} %copy.36, f32[1024,2,8,64]{3,0,2,1:T(8,128)} %copy.35, f32[1024,64]{1,0:T(8,128)S(1)} %get-tuple-element.15, f32[1024,64]{1,0:T(8,128)S(1)} %get-tuple-element.14), kind=kLoop, calls=%fused_computation.19 | loop fusion | flops 8388608 | bytes 13107200 | tf_op jit(solution)/shard_map/convert
  584.4 36.3 %fusion.28 = (f32[2,8,1024]{2,1,0:T(8,128)S(1)}, f32[2,8,1024,1024]{2,3,1,0:T(8,128)}) fusion(pred[1024,1024]{0,1:T(8,128)(4,1)S(1)} %copy-done, bf16[1024,2,8,64]{3,0,2,1:T(8,128)(2,1)} %get-tuple-element.9, bf16[1024,2,8,64]{3,0,2,1:T(8,128)(2,1)} %get-tuple-element.8, bf16[1024,2,64]{2,0,1:T(8,128)(2,1)S(1)} %get-tuple-element.13, ...), kind=kOutput, calls=%fused_computation.43 | convolution fusion | flops 4388291584 | bytes 72941568 | tf_op jit(solution)/shard_map/sub | solution.py:61
  620.7 24.1 %fusion.17 = bf16[2,128,8,1024]{3,1,2,0:T(8,128)(2,1)} fusion(f32[2,8,1024,1024]{2,3,1,0:T(8,128)} %get-tuple-element.17, f32[2,8,1024]{2,1,0:T(8,128)S(1)} %get-tuple-element.16, f32[1024,2,10,128]{0,3,2,1:T(8,128)} %bitcast.53), kind=kOutput, calls=%fused_computation.26 | convolution fusion | flops 4330618880 | bytes 71892992 | tf_op jit(solution)/shard_map/gjts,sgd->tgjd/dot_general | solution.py:63
  644.8 6.4 copy.29
  (12 shorter events, 0.1 us)
Async XLA Ops:
  7.2 292.1 %all-gather.3.cloned.1.call-start = ((), (), s32[]{:S(2)}) async-start(), calls=%async_computation.1 | async-start | bytes 20971520 | tf_op jit(solution)/shard_map/all_gather | solution.py:33
  7.9 488.4 %all-gather.5.cloned.1.call-start = ((), (), s32[]{:S(2)}) async-start(), calls=%async_computation.2 | async-start | bytes 47185920 | tf_op jit(solution)/shard_map/all_gather | solution.py:44
  87.8 8.9 %copy-start.2 = (bf16[2048]{0:T(1024)(128)(2,1)S(1)}, bf16[2048]{0:T(1024)(128)(2,1)}, u32[]{:S(2)}) copy-start(bf16[2048]{0:T(1024)(128)(2,1)} %param.5) | copy-start | bytes 12292
  87.8 33.3 %copy-start.1 = (s32[1,1024]{1,0:T(1,128)S(1)}, s32[1,1024]{1,0:T(1,128)}, u32[]{:S(2)}) copy-start(s32[1,1024]{1,0:T(1,128)} %param.7) | copy-start | bytes 12292
  574.7 9.7 %copy-start = (pred[1024,1024]{0,1:T(8,128)(4,1)S(1)}, pred[1024,1024]{0,1:T(8,128)(4,1)}, u32[]{:S(2)}) copy-start(pred[1024,1024]{0,1:T(8,128)(4,1)} %fusion.16) | copy-start | bytes 3145732
Sparse Core Ops, SparseCore 0:
  9.5 289.6 all-gather.2
  301.7 194.4 all-gather.4
where the time goes:
time: 659 us; the launch traced here: 658 us
  waiting for transfers between devices  365 us (55%)
  matrix products  115 us (17%)
  blocking collectives  89.6 us (14%)
  local copies, waits for them, and re-layouts  53.8 us (8%)
  other arithmetic  21.2 us (3%)
  between operations  14.1 us (2%)
    all_gather x1, waiting for transfers between devices, shards(): lax.all_gather(weights_rows, 'pp', axis=1, tiled=True)  190 us
    all_gather x1, waiting for transfers between devices, shards(): lax.all_gather(tokens, 'tp', axis=1, tiled=True)  174 us
    all_to_all x1, blocking collectives, shards(): lax.all_to_all(weights_gen, 'pp', split_axis=1, concat_axis=2, tiled=True)  65.3 us
    dot_general x1, matrix products, shards(): jnp.einsum('td,grd->tgr', normed, lax.all_gather(weights_rows, 'pp', axis...  54.2 us
    sub x1, matrix products, shards(): expo = jnp.where(allowed[None, None], jnp.exp(score - top), 0.0)  36.3 us
    unnamed x11, local copies, waits for them, and re-layouts  29.9 us
    all_gather x1, blocking collectives, shards(): lax.all_gather(norm_gain, 'tp', axis=0, tiled=True)  24.4 us
    dot_general x1, matrix products, shards(): jnp.einsum('gjts,sgd->tgjd', prob, value_heads, preferred_element_type=jn...  24.1 us
  transfers between devices with their start and end apart: 2, of which 2 were waited for; matrix products, arithmetic and copies ran while one was open for 4% of the time, Pallas kernels for 0%

commit v1 on v0

--- a/solution.py
+++ b/solution.py
@@ -41,7 +41,7 @@
     mixed = jnp.einsum(
         "td,grd->tgr",
         normed,
-        lax.all_gather(weights_rows, "pp", axis=1, tiled=True),
+        jnp.concatenate(lax.all_gather(weights_rows, "pp"), axis=1),
         preferred_element_type=jnp.float32,
     )
     mixed = mixed.reshape(count, groups, GROUP + 2, DH)

time: 659 us -> 631 us (0.958)
  local copies, waits for them, and re-layouts: 53.8 us -> 40.3 us
  waiting for transfers between devices: 365 us -> 356 us
    unnamed x11 -> x6, local copies, waits for them, and re-layouts: 29.9 us -> 15.8 us
    slice x2 -> x0, local copies, waits for them, and re-layouts: 9.75 us -> none  [the longest x1 8.45 us: rotary(): second = values[..., half:]]
    all_gather x0 -> x1, local copies, waits for them, and re-layouts: none -> 8.95 us  [shards(): lax.all_gather(weights_rows, 'pp')]
    all_gather x1, waiting for transfers between devices: 174 us -> 166 us  [shards(): lax.all_gather(tokens, 'tp', axis=1, tiled=True)]
where the time goes in v1:
time: 631 us; the launch traced here: 630 us
  waiting for transfers between devices  356 us (56%)
  matrix products  113 us (18%)
  blocking collectives  89.5 us (14%)
  local copies, waits for them, and re-layouts  40.3 us (6%)
  other arithmetic  16.6 us (3%)
  between operations  14.1 us (2%)
    all_gather x1, waiting for transfers between devices, shards(): lax.all_gather(weights_rows, 'pp')  189 us
    all_gather x1, waiting for transfers between devices, shards(): lax.all_gather(tokens, 'tp', axis=1, tiled=True)  166 us
    all_to_all x1, blocking collectives, shards(): lax.all_to_all(weights_gen, 'pp', split_axis=1, concat_axis=2, tiled=True)  65.3 us
    dot_general x1, matrix products, shards(): jnp.einsum('td,grd->tgr', normed, jnp.concatenate(lax.all_gather(weights_...  54.2 us
    sub x1, matrix products, shards(): expo = jnp.where(allowed[None, None], jnp.exp(score - top), 0.0)  35.1 us
    all_gather x1, blocking collectives, shards(): lax.all_gather(norm_gain, 'tp', axis=0, tiled=True)  24.3 us
    dot_general x1, matrix products, shards(): jnp.einsum('gjts,sgd->tgjd', prob, value_heads, preferred_element_type=jn...  24.2 us
    unnamed x6, local copies, waits for them, and re-layouts  15.8 us
  transfers between devices with their start and end apart: 2, of which 2 were waited for; matrix products, arithmetic and copies ran while one was open for 4% of the time, Pallas kernels for 0%

profile of v1, /device:TPU:0, one launch (start us, length us, event | category | flops | bytes accessed | tf_op | source)
XLA Modules:
  0.0 630.1 jit_solution(5889430536191746193)
XLA Ops:
  7.2 0.0 all-gather.3.cloned.1.call-start
  7.2 0.7 all-gather.3.cloned.1.call-update
  7.9 0.0 all-gather.5.cloned.1.call-start
  7.9 9.4 %copy.11 = bf16[2,1280,1024]{2,0,1:T(2,128)(2,1)S(1)} copy(bf16[2,1280,1024]{2,1,0:T(8,128)(2,1)} %param.6) | data formatting | bytes 10485760 | tf_op args[2]
  17.4 65.3 %all_to_all.18 = bf16[2,1280,1024]{2,0,1:T(2,128)(2,1)S(1)} all-to-all(bf16[2,1280,1024]{2,0,1:T(2,128)(2,1)S(1)} %copy.11), channel_id=1, replica_groups=mesh['tp'=4,'pp'=8] {'pp'}, dimensions={1} | all-to-all | bytes 10485760 | tf_op jit(solution)/shard_map/all_to_all | solution.py:31
  82.6 5.3 copy.12
  87.9 9.0 %all_gather.14 = bf16[1,2,160,8192]{3,2,0,1:T(8,128)(2,1)} reshape(bf16[2,160,8,1024]{3,2,1,0:T(8,128)(2,1)} %copy.12) | data formatting | bytes 10485760 | tf_op jit(solution)/shard_map/all_gather | solution.py:44
  96.8 0.0 all-gather.5.cloned.1.call-update
  96.9 0.0 copy-done.1
  96.9 24.3 %all_gather.13 = bf16[8192]{0:T(1024)(128)(2,1)S(1)} all-gather(bf16[2048]{0:T(1024)(128)(2,1)S(1)} %copy-done.1), channel_id=1, replica_groups=mesh['tp'=4,'pp'=8] {'tp'}, dimensions={0}, use_global_device_ids=true | all-gather | bytes 20480 | tf_op jit(solution)/shard_map/all_gather | solution.py:34
  121.2 0.5 convert_reduce_fusion
  121.7 1.0 multiply_cosine_fusion
  122.7 1.6 fusion.16
  124.2 8.9 %all_to_all.16 = bf16[2,160,8192]{2,1,0:T(8,128)(2,1)} reshape(bf16[2,160,8,1024]{3,2,1,0:T(8,128)(2,1)} %copy.12) | data formatting | bytes 10485760 | tf_op jit(solution)/shard_map/all_to_all | solution.py:31
  133.2 166.1 %all-gather.3.cloned.1.call-done = bf16[1024,8192]{1,0:T(8,128)(2,1)} async-done(((bf16[1024,2048]{1,0:T(8,128)(2,1)}), bf16[1024,8192]{1,0:T(8,128)(2,1)}) %all-gather.3.cloned.1.call-update) | async-done | bytes 16777232 | tf_op jit(solution)/shard_map/all_gather | solution.py:33
  299.3 7.2 %fusion.2 = f32[1024]{0:T(1024)S(1)} fusion(bf16[1024,8192]{1,0:T(8,128)(2,1)} %all-gather.3.cloned.1.call-done), kind=kLoop, calls=%fused_computation.7 | loop fusion | flops 25164800 | bytes 16781312 | tf_op jit(solution)/shard_map/reduce_sum | solution.py:37
  306.5 189.2 %all-gather.5.cloned.1.call-done = bf16[8,2,160,8192]{3,2,0,1:T(8,128)(2,1)} async-done(((bf16[1,2,160,8192]{3,2,0,1:T(8,128)(2,1)}), bf16[8,2,160,8192]{3,2,0,1:T(8,128)(2,1)}) %all-gather.5.cloned.1.call-update) | async-done | bytes 41943056 | tf_op jit(solution)/shard_map/all_gather | solution.py:44
  495.7 54.2 %fusion.10 = f32[1024,2,10,128]{0,3,2,1:T(8,128)} fusion(bf16[2,10,128,8192]{3,2,1,0:T(8,128)(2,1)} %bitcast.58, bf16[1024,8192]{1,0:T(8,128)(2,1)} %all-gather.3.cloned.1.call-done, f32[8192]{0:T(1024)S(1)} %convert_element_type.36, f32[1024]{0:T(1024)S(1)} %add_rsqrt_fusion), kind=kOutput, calls=%fused_computation.15 | convolution fusion | flops 42983227392 | bytes 69242880 | tf_op jit(solution)/shard_map/td,grd->tgr/dot_general | solution.py:41
  549.9 1.3 slice_bitcast_fusion
  551.2 6.2 subtract_convert_fusion
  557.4 0.2 subtract_convert_fusion.1
  557.6 35.1 %fusion.27 = (f32[2,8,1024]{2,1,0:T(8,128)S(1)}, f32[2,8,1024,1024]{2,3,1,0:T(8,128)}) fusion(pred[1024,1024]{0,1:T(8,128)(4,1)} %fusion.16, bf16[1024,2,8,64]{0,3,2,1:T(8,128)(2,1)} %get-tuple-element.7, bf16[1024,2,8,64]{0,3,2,1:T(8,128)(2,1)S(1)} %get-tuple-element.6, bf16[1024,2,64]{0,2,1:T(8,128)(2,1)S(1)} %get-tuple-element.9, ...), kind=kOutput, calls=%fused_computation.42 | convolution fusion | flops 4388291584 | bytes 72941568 | tf_op jit(solution)/shard_map/sub | solution.py:61
  592.7 24.2 %fusion.18 = bf16[2,128,8,1024]{3,1,2,0:T(8,128)(2,1)} fusion(f32[2,8,1024,1024]{2,3,1,0:T(8,128)} %get-tuple-element.13, f32[2,8,1024]{2,1,0:T(8,128)S(1)} %get-tuple-element.12, f32[1024,2,10,128]{0,3,2,1:T(8,128)} %fusion.10), kind=kOutput, calls=%fused_computation.26 | convolution fusion | flops 4330618880 | bytes 71892992 | tf_op jit(solution)/shard_map/gjts,sgd->tgjd/dot_general | solution.py:63
  616.8 6.4 %copy.17 = bf16[1024,2048]{1,0:T(8,128)(2,1)} copy(bf16[1024,2048]{0,1:T(8,128)(2,1)} %bitcast.55) | data formatting | bytes 8388608
  (7 shorter events, 0.0 us)
Async XLA Ops:
  7.2 292.1 %all-gather.3.cloned.1.call-start = ((), (), s32[]{:S(2)}) async-start(), calls=%async_computation.1 | async-start | bytes 20971520 | tf_op jit(solution)/shard_map/all_gather | solution.py:33
  7.9 487.8 %all-gather.5.cloned.1.call-start = ((), (), s32[]{:S(2)}) async-start(), calls=%async_computation.2 | async-start | bytes 47185920 | tf_op jit(solution)/shard_map/all_gather | solution.py:44
  87.9 9.0 %copy-start.1 = (bf16[2048]{0:T(1024)(128)(2,1)S(1)}, bf16[2048]{0:T(1024)(128)(2,1)}, u32[]{:S(2)}) copy-start(bf16[2048]{0:T(1024)(128)(2,1)} %param.5) | copy-start | bytes 12292
  87.9 33.3 %copy-start = (s32[1,1024]{1,0:T(1,128)S(1)}, s32[1,1024]{1,0:T(1,128)}, u32[]{:S(2)}) copy-start(s32[1,1024]{1,0:T(1,128)} %param.7) | copy-start | bytes 12292
Sparse Core Ops, SparseCore 0:
  9.5 289.6 all-gather.2
  301.2 194.4 all-gather.4
